TPU v7x, 32 devices: a whole 2x2x4 slice. The times are simulated.
32 devices in a mesh: ctx: 8 (over z, x), tp: 4 (over y, core).
Axes of the slice: x: 2, y: 2, z: 4, core: 2. Of those that a mesh axis runs over, the one named last changes fastest.
Arguments:
- queries: bfloat16 [2048, 8192], P('ctx', 'tp'), may hold values from -8 to 8
- keys: bfloat16 [2048, 1024], P('ctx'), may hold values from -7 to 7
- values: bfloat16 [2048, 1024], P('ctx'), may hold values from -6 to 6
- out_weight: bfloat16 [8192, 4096], P('tp'), may hold values from -0.25 to 0.25
- block_order: int32 [16], P('ctx'), may hold values from 0 to 15, each once
Outputs:
- projected: bfloat16 [2048, 4096], P('ctx', 'tp')
Inputs may be any that keep to these rules, and one draw needn't show every extreme that they name: `block_order`: every sequence block appears exactly once.
All inputs are finite; a program needn't handle non-finite values.
Results may differ from a plain program's by a relative error of at most 0.015.
Values may be sent and summed in bfloat16 or wider, within the bound.
A program may use at most 64 MiB of HBM per device.

v0:
```python
import functools
import math

import jax
import jax.numpy as jnp
from jax import lax
from jax.experimental import pallas as pl
from jax.experimental.pallas import tpu as pltpu
from jax.sharding import PartitionSpec as P

QUERY_HEADS = 64
KEY_VALUE_HEADS = 8
HEAD_SIZE = 128
MESH = pl.DeviceIdType.MESH
NT = (((1,), (1,)), ((), ()))


def kernel(dims, q_hbm, k_hbm, v_hbm, w_hbm, order, o_ref, q, w, kv, orders, mask, eye, scores,
           att, pair_out, pair_in, far_out, far_in, load_sem, send, recv,
           pair_send, pair_recv, far_send, far_recv):
    n, tp, rows, heads, kv_heads, unit, wide = dims
    line, groups = n // 2, tp // 2
    tokens = n * rows
    blocks = rows // 128
    per_kv = heads // kv_heads
    me, t = lax.axis_index("ctx"), lax.axis_index("tp")
    a, b = me // 2, lax.rem(me, 2)
    y, c = t // 2, lax.rem(t, 2)
    other = 1 - b
    partner = (me, y * 2 + 1 - c)

    def far(i):
        return lax.rem(y + i, groups)

    first = t * heads // (QUERY_HEADS // KEY_VALUE_HEADS)
    own = pl.ds(pl.multiple_of(me * rows, 128), rows)
    loads = []
    for p in range(2 * kv_heads):
        src = v_hbm if p % 2 else k_hbm
        cols = pl.ds(pl.multiple_of((first + p // 2) * HEAD_SIZE, 128), HEAD_SIZE)
        loads.append(pltpu.make_async_copy(src.at[:, cols], kv.at[p, own, :], load_sem.at[p]))
        loads[-1].start()
    q_load = pltpu.make_async_copy(q_hbm, q, load_sem.at[2 * kv_heads])
    w_load = pltpu.make_async_copy(w_hbm, w, load_sem.at[2 * kv_heads + 1])
    q_load.start()
    w_load.start()
    for i in range(blocks):
        orders[pl.ds(me, 1), i:i + 1, :] = jnp.full((1, 1, 128), order[i], jnp.int32)

    def guarded(cond, act):
        pl.when(cond)(act)

    up, down, across = a + 1 < line, a > 0, a * 2 + other

    barrier = pltpu.get_barrier_semaphore()

    def greet(target):
        pl.semaphore_signal(barrier, inc=1, device_id=target, device_id_type=MESH)

    guarded(up, lambda: greet((me + 2, t)))
    guarded(down, lambda: greet((me - 2, t)))
    greet((across, t))
    greet(partner)
    for i in range(1, groups):
        greet((me, far(i) * 2 + c))
    pl.semaphore_wait(barrier, 1 + groups + up.astype(jnp.int32) + down.astype(jnp.int32))

    marks = 2 * kv_heads

    def piece(p, block, way, target):
        at = pl.ds(pl.multiple_of(block * rows, 128), rows)
        ref = orders.at[block] if p == marks else kv.at[p, at, :]
        return pltpu.make_async_remote_copy(
            src_ref=ref, dst_ref=ref, send_sem=send.at[p, block, way],
            recv_sem=recv.at[p, block], device_id=(target, t), device_id_type=MESH)

    def open_own(p):
        if p != marks:
            loads[p].wait()
        guarded(up, lambda: piece(p, me, 0, me + 2).start())
        guarded(down, lambda: piece(p, me, 1, me - 2).start())
        piece(p, me, 2, across).start()

    def relay(p, s):
        low, high = me - 2 * s, me + 2 * s

        @pl.when(a - s >= 0)
        def _():
            piece(p, low, 0, me).wait_recv()
            guarded(up, lambda: piece(p, low, 0, me + 2).start())
            piece(p, low, 2, across).start()

        @pl.when(a + s < line)
        def _():
            piece(p, high, 1, me).wait_recv()
            guarded(down, lambda: piece(p, high, 1, me - 2).start())
            piece(p, high, 2, across).start()

    def step(h, s):
        for p in (2 * h, 2 * h + 1):
            relay(p, s)

    def finish(h):
        def body(i, _):
            for p in (2 * h, 2 * h + 1):
                piece(p, i * 2 + other, 2, me).wait_recv()
            return 0
        lax.fori_loop(0, line, body, 0)

    row = lax.broadcasted_iota(jnp.int32, (128, 128), 0)
    col = lax.broadcasted_iota(jnp.int32, (128, 128), 1)

    def build(i):
        for j in range(blocks):
            kpos = orders[pl.ds(i, 1), j:j + 1, :][0] * 128 + row
            for g in range(blocks):
                qpos = orders[pl.ds(me, 1), g:g + 1, :][0] * 128 + col
                at = pl.ds(pl.multiple_of(i * rows + j * 128, 128), 128)
                mask[g, at, :] = jnp.where(kpos <= qpos, 0.0, -1e30).astype(jnp.bfloat16)

    def build_crossed(s):
        def one(i):
            piece(marks, i, 2, me).wait_recv()
            build(i)
        guarded(a - s >= 0, lambda: one(across - 2 * s))
        guarded(jnp.logical_and(s > 0, a + s < line), lambda: one(across + 2 * s))

    open_own(marks)
    early = 2 if line > 2 else 2 * kv_heads
    for p in range(early):
        open_own(p)
    eye[...] = (row == col).astype(jnp.bfloat16)
    build(me)

    def first_head(s, _):
        relay(marks, s)
        step(0, s)
        if kv_heads > 1:
            for p in range(early, 2 * kv_heads):
                guarded(s == min(p - 1, 2), lambda p=p: open_own(p))
        guarded(a - s >= 0, lambda: build(me - 2 * s))
        guarded(a + s < line, lambda: build(me + 2 * s))
        build_crossed(s - 1)
        return 0
    lax.fori_loop(1, line, first_head, 0)
    if kv_heads > 1 and line > 2:
        step(1, 1)
    build_crossed(jnp.int32(line - 1))
    finish(0)
    if kv_heads > 1:
        for s in range(2, line - 1):
            step(1, s)
    q_load.wait()

    chunk = tokens // 4
    factor = math.log2(math.e) / math.sqrt(HEAD_SIZE)
    ones = jnp.ones((chunk, 128), jnp.bfloat16)
    per_block = per_kv // unit

    def attend(h, g, u):
        at = pl.ds(pl.multiple_of(g * 128, 128), 128)
        def head_cols(k):
            return pl.ds(pl.multiple_of((h * per_kv + u * unit + k) * HEAD_SIZE, 128), HEAD_SIZE)
        e = eye[...]
        qa = jnp.concatenate(
            [jnp.concatenate([q[at, head_cols(k)], e], axis=1) for k in range(unit)], axis=0)
        top = None
        for i in range(4):
            ks = pl.ds(i * chunk, chunk)
            ka = jnp.concatenate([kv[2 * h, ks, :], mask[g, ks, :]], axis=1)
            s = lax.dot_general(qa, ka, NT, preferred_element_type=jnp.float32)
            scores[:, ks] = s
            for j in range(0, chunk, 128):
                part = s[:, j:j + 128]
                top = part if top is None else jnp.maximum(top, part)
        top = jnp.max(top, axis=1, keepdims=True)
        acc = None
        for i in range(4):
            ks = pl.ds(i * chunk, chunk)
            weight = jnp.exp2((scores[:, ks] - top) * factor).astype(jnp.bfloat16)
            va = jnp.concatenate([kv[2 * h + 1, ks, :], ones], axis=1)
            part = jnp.dot(weight, va, preferred_element_type=jnp.float32)
            acc = part if acc is None else acc + part
        res = (acc[:, :128] / acc[:, 128:]).astype(jnp.bfloat16)
        for k in range(unit):
            att[at, head_cols(k)] = res[k * 128:(k + 1) * 128]

    total = blocks * per_block
    for h in range(kv_heads):
        def body(i, _):
            attend(h, i // per_block, lax.rem(i, per_block))
            if h == 0 and kv_heads > 1:
                guarded(i == 0, lambda: step(1, line - 1))
            return 0
        lax.fori_loop(0, total, body, 0)
        if h + 1 < kv_heads:
            for s in range(1 if h else line - 1, line) if (h or total < 2) else ():
                step(h + 1, s)
            finish(h + 1)

    quarter = o_ref.shape[1]
    parts = quarter // wide
    w_load.wait()

    def product(group, core, j):
        cols = pl.ds(pl.multiple_of((group * 2 + core) * quarter + j * wide, 128), wide)
        return jnp.dot(att[...], w[:, cols], preferred_element_type=jnp.float32)

    def pair_copy(i, j):
        return pltpu.make_async_remote_copy(
            src_ref=pair_out.at[i, j], dst_ref=pair_in.at[i, j], send_sem=pair_send.at[i, j],
            recv_sem=pair_recv.at[i, j], device_id=partner, device_id_type=MESH)

    def far_copy(i, j):
        return pltpu.make_async_remote_copy(
            src_ref=far_out.at[i, j], dst_ref=far_in.at[i, j], send_sem=far_send.at[i, j],
            recv_sem=far_recv.at[i, j], device_id=(me, far(i) * 2 + c), device_id_type=MESH)

    def far_step(k, _):
        i, j = 1 + k // parts, lax.rem(k, parts)
        pair_out[i, j] = product(far(i), 1 - c, j).astype(jnp.bfloat16)
        pair_copy(i, j).start()
        mine = product(far(i), c, j)
        pair_copy(i, j).wait_recv()
        far_out[i, j] = (mine + pair_in[i, j].astype(jnp.float32)).astype(jnp.bfloat16)
        far_copy(i, j).start()
        return 0
    lax.fori_loop(0, (groups - 1) * parts, far_step, 0)

    def near_step(j, _):
        pair_out[0, j] = product(y, 1 - c, j).astype(jnp.bfloat16)
        pair_copy(0, j).start()
        far_out[0, j] = product(y, c, j).astype(jnp.bfloat16)
        return 0
    lax.fori_loop(0, parts, near_step, 0)

    def close_step(j, _):
        pair_copy(0, j).wait_recv()
        res = far_out[0, j].astype(jnp.float32) + pair_in[0, j].astype(jnp.float32)
        for i in range(1, groups):
            far_copy(i, j).wait_recv()
            res = res + far_in[i, j].astype(jnp.float32)
        o_ref[:, pl.ds(pl.multiple_of(j * wide, 128), wide)] = res.astype(jnp.bfloat16)
        return 0
    lax.fori_loop(0, parts, close_step, 0)

    def drain(i, _):
        for p in range(2 * kv_heads + 1):
            blk = i * 2 + b
            guarded(jnp.logical_and(up, i <= a), lambda: piece(p, blk, 0, me + 2).wait_send())
            guarded(jnp.logical_and(down, i >= a), lambda: piece(p, blk, 1, me - 2).wait_send())
            piece(p, blk, 2, across).wait_send()
        return 0
    lax.fori_loop(0, line, drain, 0)

    def drain_out(j, _):
        for i in range(groups):
            pair_copy(i, j).wait_send()
            if i:
                far_copy(i, j).wait_send()
        return 0
    lax.fori_loop(0, parts, drain_out, 0)


def shards(n, tp, queries, keys, values, out_weight, block_order):
    rows = queries.shape[0]
    heads = queries.shape[1] // HEAD_SIZE
    group = QUERY_HEADS // KEY_VALUE_HEADS
    kv_heads = max(1, heads // group)
    unit = min(4, heads // kv_heads)
    quarter = out_weight.shape[1] // tp
    wide = min(256, quarter)
    parts, groups, tokens, blocks = quarter // wide, tp // 2, n * rows, rows // 128
    dims = (n, tp, rows, heads, kv_heads, unit, wide)
    any_space = pl.BlockSpec(memory_space=pl.ANY)
    dma = pltpu.SemaphoreType.DMA
    bf16 = jnp.bfloat16
    swap = pltpu.VMEM((groups, parts, rows, wide), bf16)
    return pl.pallas_call(
        functools.partial(kernel, dims),
        out_shape=jax.ShapeDtypeStruct((rows, quarter), bf16),
        in_specs=[any_space] * 4 + [pl.BlockSpec(memory_space=pltpu.SMEM)],
        out_specs=pl.BlockSpec(memory_space=pltpu.VMEM),
        scratch_shapes=[
            pltpu.VMEM(queries.shape, bf16),
            pltpu.VMEM(out_weight.shape, bf16),
            pltpu.VMEM((2 * kv_heads, tokens, HEAD_SIZE), bf16),
            pltpu.VMEM((n, 8, 128), jnp.int32),
            pltpu.VMEM((blocks, tokens, 128), bf16),
            pltpu.VMEM((128, 128), bf16),
            pltpu.VMEM((unit * 128, tokens), jnp.float32),
            pltpu.VMEM((rows, heads * HEAD_SIZE), bf16),
            swap, swap, swap, swap,
            dma((2 * kv_heads + 2,)),
            dma((2 * kv_heads + 1, n, 3)), dma((2 * kv_heads + 1, n)),
            dma((groups, parts)), dma((groups, parts)), dma((groups, parts)), dma((groups, parts)),
        ],
        compiler_params=pltpu.CompilerParams(
            collective_id=0, has_side_effects=True, vmem_limit_bytes=60 * 2**20),
    )(queries, keys, values, out_weight, block_order)


def solution(mesh):
    n, tp = mesh.shape["ctx"], mesh.shape["tp"]
    in_specs = (P("ctx", "tp"), P("ctx", None), P("ctx", None), P("tp", None), P("ctx"))
    return jax.shard_map(functools.partial(shards, n, tp), mesh=mesh, in_specs=in_specs,
                         out_specs=P("ctx", "tp"), check_vma=False)
```

profile of v0, /device:TPU:0, one launch (start us, length us, event | category | flops | bytes accessed | tf_op | source)
XLA Modules:
  0.0 63.1 jit_solution(9213495131322085448)
XLA Ops:
  0.0 61.3 %shard_map.55 = bf16[256,1024]{1,0:T(8,128)(2,1)} custom-call(bf16[256,2048]{1,0:T(8,128)(2,1)} %q_hbm.1, bf16[256,1024]{1,0:T(8,128)(2,1)} %k_hbm.1, bf16[256,1024]{1,0:T(8,128)(2,1)} %v_hbm.1, bf16[2048,4096]{1,0:T(8,128)(2,1)} %w_hbm.1, s32[2]{0:T(128)} %order.1), custom_call_target="tpu_custom_call" | custom-call | tf_op jit(solution)/shard_map/pallas_call | solution.py:279
  61.3 1.9 %copy.7 = bf16[256,1024]{1,0:T(8,128)(2,1)} copy(bf16[256,1024]{1,0:T(8,128)(2,1)} %shard_map.55) | data formatting | bytes 1048576
where the time goes:
time: 63.3 us; the launch traced here: 63.1 us
  Pallas kernels  61.3 us (97%)
  local copies, waits for them, and re-layouts  1.87 us (3%)
    pallas_call x1, Pallas kernels, shards(): pl.pallas_call(functools.partial(kernel, dims), out_shape=jax.ShapeDtypeS...  61.3 us
    unnamed x1, local copies, waits for them, and re-layouts  1.87 us

commit v1 on v0

v1 whole, which is shorter than its diff:
```python
import functools
import math

import jax
import jax.numpy as jnp
from jax import lax
from jax.experimental import pallas as pl
from jax.experimental.pallas import tpu as pltpu
from jax.sharding import PartitionSpec as P

QUERY_HEADS = 64
KEY_VALUE_HEADS = 8
HEAD_SIZE = 128
MESH = pl.DeviceIdType.MESH
NT = (((1,), (1,)), ((), ()))


def kernel(dims, q_hbm, k_hbm, v_hbm, w_hbm, order, o_ref, q, w, kv, orders, mask, eye, scores,
           top, acc, pair_out, pair_in, far_out, far_in, load_sem, send, recv,
           pair_send, pair_recv, far_send, far_recv):
    n, tp, rows, heads, kv_heads, wide = dims
    line, groups = n // 2, tp // 2
    blocks = rows // 128
    per_kv = heads // kv_heads
    tile = per_kv * 128
    me, t = lax.axis_index("ctx"), lax.axis_index("tp")
    a, b = me // 2, lax.rem(me, 2)
    y, c = t // 2, lax.rem(t, 2)
    other = 1 - b
    partner = (me, y * 2 + 1 - c)

    def far(i):
        return lax.rem(y + i, groups)

    first = t * heads // (QUERY_HEADS // KEY_VALUE_HEADS)
    own = pl.ds(pl.multiple_of(me * rows, 128), rows)
    key_parts = range(0, 2 * kv_heads, 2)
    value_parts = range(1, 2 * kv_heads, 2)
    loads = {}
    for p in (*key_parts, *value_parts):
        src = v_hbm if p % 2 else k_hbm
        cols = pl.ds(pl.multiple_of((first + p // 2) * HEAD_SIZE, 128), HEAD_SIZE)
        loads[p] = pltpu.make_async_copy(src.at[:, cols], kv.at[p, own, :], load_sem.at[p])
        loads[p].start()
    q_load = pltpu.make_async_copy(q_hbm, q, load_sem.at[2 * kv_heads])
    w_load = pltpu.make_async_copy(w_hbm, w, load_sem.at[2 * kv_heads + 1])
    q_load.start()
    for i in range(blocks):
        orders[pl.ds(me, 1), i:i + 1, :] = jnp.full((1, 1, 128), order[i], jnp.int32)

    def guarded(cond, act):
        pl.when(cond)(act)

    up, down, across = a + 1 < line, a > 0, a * 2 + other

    barrier = pltpu.get_barrier_semaphore()

    def greet(target):
        pl.semaphore_signal(barrier, inc=1, device_id=target, device_id_type=MESH)

    guarded(up, lambda: greet((me + 2, t)))
    guarded(down, lambda: greet((me - 2, t)))
    greet((across, t))
    greet(partner)
    for i in range(1, groups):
        greet((me, far(i) * 2 + c))
    pl.semaphore_wait(barrier, 1 + groups + up.astype(jnp.int32) + down.astype(jnp.int32))

    marks = 2 * kv_heads

    def piece(p, block, way, target):
        at = pl.ds(pl.multiple_of(block * rows, 128), rows)
        ref = orders.at[block] if p == marks else kv.at[p, at, :]
        return pltpu.make_async_remote_copy(
            src_ref=ref, dst_ref=ref, send_sem=send.at[p, block, way],
            recv_sem=recv.at[p, block], device_id=(target, t), device_id_type=MESH)

    def send_up(p, block):
        piece(p, block, 0, me + 2).start()

    def send_down(p, block):
        piece(p, block, 1, me - 2).start()

    def send_across(p, block):
        piece(p, block, 2, across).start()

    def arrived(p, block):
        piece(p, block, 2, me).wait_recv()

    def column(i):
        near = jnp.minimum(a, line - 1 - a)
        s = (i + 1) // 2
        zigzag = jnp.where(lax.rem(i, 2) == 1, a - s, a + s)
        onward = jnp.where(a < line - 1 - a, i, line - 1 - i)
        return jnp.where(i <= 2 * near, zigzag, onward)

    def onward(p, block):
        z = block // 2
        guarded(jnp.logical_and(up, z <= a), lambda: send_up(p, block))
        guarded(jnp.logical_and(down, z >= a), lambda: send_down(p, block))

    def near(i):
        return column(i) * 2 + b

    def crossed(i):
        return column(i) * 2 + other

    row = lax.broadcasted_iota(jnp.int32, (128, 128), 0)
    col = lax.broadcasted_iota(jnp.int32, (128, 128), 1)

    def build(i):
        for j in range(blocks):
            kpos = orders[pl.ds(i, 1), j:j + 1, :][0] * 128 + row
            for g in range(blocks):
                qpos = orders[pl.ds(me, 1), g:g + 1, :][0] * 128 + col
                at = pl.ds(pl.multiple_of(i * rows + j * 128, 128), 128)
                mask[g, at, :] = jnp.where(kpos <= qpos, 0.0, -1e30).astype(jnp.bfloat16)

    for p in (marks, *key_parts):
        if p != marks:
            loads[p].wait()
        onward(p, me)
        send_across(p, me)
    for p in value_parts:
        loads[p].wait()
        onward(p, me)
    send_across(1, me)
    w_load.start()
    eye[...] = (row == col).astype(jnp.bfloat16)
    top[...] = jnp.full(top.shape, -3e38, jnp.float32)
    q_load.wait()

    factor = math.log2(math.e) / math.sqrt(HEAD_SIZE)

    def score(slot, block):
        at = pl.ds(pl.multiple_of(block * rows, 128), rows)
        e = eye[...]
        for h in range(kv_heads):
            for g in range(blocks):
                ka = jnp.concatenate([kv[2 * h, at, :], mask[g, at, :]], axis=1)
                qa = jnp.concatenate(
                    [jnp.concatenate([q[g * 128:(g + 1) * 128, m * 128:(m + 1) * 128], e], axis=1)
                     for m in range(h * per_kv, (h + 1) * per_kv)], axis=0)
                s = lax.dot_general(qa, ka, NT, preferred_element_type=jnp.float32) * factor
                to = slice((h * blocks + g) * tile, (h * blocks + g + 1) * tile)
                scores[slot, to, :] = s
                best = top[to, :]
                for j in range(0, rows, 128):
                    best = jnp.maximum(best, s[:, j:j + 128])
                top[to, :] = best

    def relay_keys(i):
        for p in (marks, *key_parts):
            arrived(p, near(i))
            onward(p, near(i))
            send_across(p, near(i))
        build(near(i))

    def relay_values(i):
        for p in value_parts:
            arrived(p, near(i))
            onward(p, near(i))
        for p in value_parts:
            send_across(p, near(i))

    def take_keys(i):
        for p in (marks, *key_parts):
            arrived(p, crossed(i))
        build(crossed(i))

    build(me)
    score(0, me)
    for i in range(1, line):
        relay_keys(i)
        if i > 1:
            relay_values(i - 1)
            score(2 * i - 3, crossed(i - 2))
        else:
            take_keys(0)
            for p in value_parts[1:]:
                send_across(p, me)
        score(2 * i, near(i))
        if i > 1:
            take_keys(i - 1)
    score(2 * line - 3, crossed(line - 2))
    relay_values(line - 1)
    take_keys(line - 1)
    score(2 * line - 1, crossed(line - 1))

    def settle(i, _):
        at = pl.ds(pl.multiple_of(i * tile, 128), tile)
        top[at, :] = jnp.broadcast_to(jnp.max(top[at, :], axis=1, keepdims=True), (tile, 128))
        return 0
    lax.fori_loop(0, kv_heads * blocks, settle, 0)
    acc[...] = jnp.zeros(acc.shape, jnp.float32)

    ones = jnp.ones((2 * rows, 128), jnp.bfloat16)

    def value_step(i, _):
        block, over = near(i), crossed(i)
        for p in value_parts:
            arrived(p, over)
        for h in range(kv_heads):
            va = jnp.concatenate([
                jnp.concatenate([kv[2 * h + 1, pl.ds(pl.multiple_of(block * rows, 128), rows), :],
                                 kv[2 * h + 1, pl.ds(pl.multiple_of(over * rows, 128), rows), :]],
                                axis=0), ones], axis=1)
            for g in range(blocks):
                to = slice((h * blocks + g) * tile, (h * blocks + g + 1) * tile)
                best = top[to, :]
                weight = jnp.concatenate(
                    [jnp.exp2(scores[2 * i + x, to, j:j + 128] - best).astype(jnp.bfloat16)
                     for x in range(2) for j in range(0, rows, 128)], axis=1)
                acc[to, :] += jnp.dot(weight, va, preferred_element_type=jnp.float32)
        return 0
    lax.fori_loop(0, line, value_step, 0)

    att = q
    for h in range(kv_heads):
        for g in range(blocks):
            for m in range(per_kv):
                at = ((h * blocks + g) * per_kv + m) * 128
                res = acc[at:at + 128, :128] / acc[at:at + 128, 128:]
                cols = (h * per_kv + m) * 128
                att[g * 128:(g + 1) * 128, cols:cols + 128] = res.astype(jnp.bfloat16)

    quarter = o_ref.shape[1]
    parts = quarter // wide
    w_load.wait()

    def product(group, core, j):
        cols = pl.ds(pl.multiple_of((group * 2 + core) * quarter + j * wide, 128), wide)
        return jnp.dot(att[...], w[:, cols], preferred_element_type=jnp.float32)

    def pair_copy(i, j):
        return pltpu.make_async_remote_copy(
            src_ref=pair_out.at[i, j], dst_ref=pair_in.at[i, j], send_sem=pair_send.at[i, j],
            recv_sem=pair_recv.at[i, j], device_id=partner, device_id_type=MESH)

    def far_copy(i, j):
        return pltpu.make_async_remote_copy(
            src_ref=far_out.at[i - 1, j], dst_ref=far_in.at[i - 1, j], send_sem=far_send.at[i, j],
            recv_sem=far_recv.at[i, j], device_id=(me, far(i) * 2 + c), device_id_type=MESH)

    def far_step(k, _):
        i, j = 1 + k // parts, lax.rem(k, parts)
        pair_out[i, j] = product(far(i), 1 - c, j).astype(jnp.bfloat16)
        pair_copy(i, j).start()
        mine = product(far(i), c, j)
        pair_copy(i, j).wait_recv()
        far_out[i - 1, j] = (mine + pair_in[i, j].astype(jnp.float32)).astype(jnp.bfloat16)
        far_copy(i, j).start()
        return 0
    lax.fori_loop(0, (groups - 1) * parts, far_step, 0)

    def near_rows(j):
        return pl.ds(pl.multiple_of(j * rows, 128), rows)

    def near_step(j, _):
        pair_out[0, j] = product(y, 1 - c, j).astype(jnp.bfloat16)
        pair_copy(0, j).start()
        acc[near_rows(j), :wide] = product(y, c, j)
        return 0
    lax.fori_loop(0, parts, near_step, 0)

    def close_step(j, _):
        pair_copy(0, j).wait_recv()
        res = acc[near_rows(j), :wide] + pair_in[0, j].astype(jnp.float32)
        for i in range(1, groups):
            far_copy(i, j).wait_recv()
            res = res + far_in[i - 1, j].astype(jnp.float32)
        o_ref[:, pl.ds(pl.multiple_of(j * wide, 128), wide)] = res.astype(jnp.bfloat16)
        return 0
    lax.fori_loop(0, parts, close_step, 0)

    def drain(i, _):
        for p in range(2 * kv_heads + 1):
            blk = i * 2 + b
            guarded(jnp.logical_and(up, i <= a), lambda: piece(p, blk, 0, me + 2).wait_send())
            guarded(jnp.logical_and(down, i >= a), lambda: piece(p, blk, 1, me - 2).wait_send())
            piece(p, blk, 2, across).wait_send()
        return 0
    lax.fori_loop(0, line, drain, 0)

    def drain_out(j, _):
        for i in range(groups):
            pair_copy(i, j).wait_send()
            if i:
                far_copy(i, j).wait_send()
        return 0
    lax.fori_loop(0, parts, drain_out, 0)


def shards(n, tp, queries, keys, values, out_weight, block_order):
    rows = queries.shape[0]
    heads = queries.shape[1] // HEAD_SIZE
    group = QUERY_HEADS // KEY_VALUE_HEADS
    kv_heads = max(1, heads // group)
    quarter = out_weight.shape[1] // tp
    wide = min(256, quarter)
    parts, groups, tokens, blocks = quarter // wide, tp // 2, n * rows, rows // 128
    dims = (n, tp, rows, heads, kv_heads, wide)
    any_space = pl.BlockSpec(memory_space=pl.ANY)
    dma = pltpu.SemaphoreType.DMA
    bf16 = jnp.bfloat16
    swap = pltpu.VMEM((groups, parts, rows, wide), bf16)
    swap_far = pltpu.VMEM((groups - 1, parts, rows, wide), bf16)
    return pl.pallas_call(
        functools.partial(kernel, dims),
        out_shape=jax.ShapeDtypeStruct((rows, quarter), bf16),
        in_specs=[any_space] * 4 + [pl.BlockSpec(memory_space=pltpu.SMEM)],
        out_specs=pl.BlockSpec(memory_space=pltpu.VMEM),
        scratch_shapes=[
            pltpu.VMEM(queries.shape, bf16),
            pltpu.VMEM(out_weight.shape, bf16),
            pltpu.VMEM((2 * kv_heads, tokens, HEAD_SIZE), bf16),
            pltpu.VMEM((n, 8, 128), jnp.int32),
            pltpu.VMEM((blocks, tokens, 128), bf16),
            pltpu.VMEM((128, 128), bf16),
            pltpu.VMEM((n, heads * rows, rows), jnp.float32),
            pltpu.VMEM((heads * rows, 128), jnp.float32),
            pltpu.VMEM((heads * rows, 256), jnp.float32),
            swap, swap, swap_far, swap_far,
            dma((2 * kv_heads + 2,)),
            dma((2 * kv_heads + 1, n, 3)), dma((2 * kv_heads + 1, n)),
            dma((groups, parts)), dma((groups, parts)), dma((groups, parts)), dma((groups, parts)),
        ],
        compiler_params=pltpu.CompilerParams(
            collective_id=0, has_side_effects=True, vmem_limit_bytes=67043328),
    )(queries, keys, values, out_weight, block_order)


def solution(mesh):
    n, tp = mesh.shape["ctx"], mesh.shape["tp"]
    in_specs = (P("ctx", "tp"), P("ctx", None), P("ctx", None), P("tp", None), P("ctx"))
    return jax.shard_map(functools.partial(shards, n, tp), mesh=mesh, in_specs=in_specs,
                         out_specs=P("ctx", "tp"), check_vma=False)
```

time: 63.3 us -> 53.3 us (0.84)
  Pallas kernels: 61.3 us -> 51.2 us
    pallas_call x1, Pallas kernels: 61.3 us -> 51.2 us  [shards(): pl.pallas_call(functools.partial(kernel, dims), out_shape=jax.ShapeDtypeS...]
where the time goes in v1:
time: 53.3 us; the launch traced here: 53.1 us
  Pallas kernels  51.2 us (96%)
  local copies, waits for them, and re-layouts  1.87 us (4%)
    pallas_call x1, Pallas kernels, shards(): pl.pallas_call(functools.partial(kernel, dims), out_shape=jax.ShapeDtypeS...  51.2 us
    unnamed x1, local copies, waits for them, and re-layouts  1.87 us

profile of v1, /device:TPU:0, one launch (start us, length us, event | category | flops | bytes accessed | tf_op | source)
XLA Modules:
  0.0 53.1 jit_solution(2699119084734161023)
XLA Ops:
  0.0 51.2 %shard_map.55 = bf16[256,1024]{1,0:T(8,128)(2,1)} custom-call(bf16[256,2048]{1,0:T(8,128)(2,1)} %q_hbm.1, bf16[256,1024]{1,0:T(8,128)(2,1)} %k_hbm.1, bf16[256,1024]{1,0:T(8,128)(2,1)} %v_hbm.1, bf16[2048,4096]{1,0:T(8,128)(2,1)} %w_hbm.1, s32[2]{0:T(128)} %order.1), custom_call_target="tpu_custom_call" | custom-call | tf_op jit(solution)/shard_map/pallas_call | solution.py:308
  51.2 1.9 %copy.7 = bf16[256,1024]{1,0:T(8,128)(2,1)} copy(bf16[256,1024]{1,0:T(8,128)(2,1)} %shard_map.55) | data formatting | bytes 1048576

commit v2 on v1

--- a/solution.py
+++ b/solution.py
@@ -127,12 +127,24 @@
     send_across(1, me)
     w_load.start()
     eye[...] = (row == col).astype(jnp.bfloat16)
-    top[...] = jnp.full(top.shape, -3e38, jnp.float32)
     q_load.wait()
 
     factor = math.log2(math.e) / math.sqrt(HEAD_SIZE)
 
-    def score(slot, block):
+    half = line // 2
+
+    last = line - 1
+
+    def near_slot(i):
+        return 2 * i if i < last else 0
+
+    def crossed_slot(i):
+        return 2 * i + 1 if i < last - 1 else i - last + 2
+
+    def span(h, g):
+        return slice((h * blocks + g) * tile, (h * blocks + g + 1) * tile)
+
+    def score(place, block, side, fresh=False):
         at = pl.ds(pl.multiple_of(block * rows, 128), rows)
         e = eye[...]
         for h in range(kv_heads):
@@ -142,12 +154,18 @@
                     [jnp.concatenate([q[g * 128:(g + 1) * 128, m * 128:(m + 1) * 128], e], axis=1)
                      for m in range(h * per_kv, (h + 1) * per_kv)], axis=0)
                 s = lax.dot_general(qa, ka, NT, preferred_element_type=jnp.float32) * factor
-                to = slice((h * blocks + g) * tile, (h * blocks + g + 1) * tile)
-                scores[slot, to, :] = s
-                best = top[to, :]
+                to = span(h, g)
+                scores[place, to, :] = s
+                best = None if fresh else top[side, to, :]
                 for j in range(0, rows, 128):
-                    best = jnp.maximum(best, s[:, j:j + 128])
-                top[to, :] = best
+                    best = s[:, j:j + 128] if best is None else jnp.maximum(best, s[:, j:j + 128])
+                top[side, to, :] = best
+
+    def score_near(i):
+        score(near_slot(i), near(i), i // half, i % half == 0)
+
+    def score_crossed(i):
+        score(crossed_slot(i), crossed(i), i // half)
 
     def relay_keys(i):
         for p in (marks, *key_parts):
@@ -160,6 +178,8 @@
         for p in value_parts:
             arrived(p, near(i))
             onward(p, near(i))
+
+    def cross_values(i):
         for p in value_parts:
             send_across(p, near(i))
 
@@ -168,110 +188,165 @@
             arrived(p, crossed(i))
         build(crossed(i))
 
+    def take_values(i):
+        for p in value_parts:
+            arrived(p, crossed(i))
+
+    def peak(side, at):
+        return jnp.broadcast_to(jnp.max(top[side, at, :], axis=1, keepdims=True), (tile, 128))
+
+    def settle_first():
+        def body(i, _):
+            at = pl.ds(pl.multiple_of(i * tile, 128), tile)
+            top[0, at, :] = peak(0, at)
+            return 0
+        lax.fori_loop(0, kv_heads * blocks, body, 0)
+
+    def settle_second():
+        def body(i, _):
+            at = pl.ds(pl.multiple_of(i * tile, 128), tile)
+            before = top[0, at, :]
+            after = jnp.maximum(before, peak(1, at))
+            top[1, at, :] = after
+            shrink = jnp.exp2(before - after)
+            acc[at, :] = acc[at, :] * jnp.concatenate([shrink, shrink], axis=1)
+            return 0
+        lax.fori_loop(0, kv_heads * blocks, body, 0)
+
+    def summed(h, g, pieces, side):
+        to = span(h, g)
+        best = top[side, to, :]
+        weight = jnp.concatenate(
+            [jnp.exp2(scores[place, to, j:j + 128] - best).astype(jnp.bfloat16)
+             for place, _ in pieces for j in range(0, rows, 128)], axis=1)
+        va = jnp.concatenate([kv[2 * h + 1, pl.ds(pl.multiple_of(block * rows, 128), rows), :]
+                              for _, block in pieces], axis=0)
+        va = jnp.concatenate([va, jnp.ones(va.shape, jnp.bfloat16)], axis=1)
+        return jnp.dot(weight, va, preferred_element_type=jnp.float32)
+
+    def absorb(pieces, side, fresh=False):
+        for h in range(kv_heads):
+            for g in range(blocks):
+                part = summed(h, g, pieces, side)
+                acc[span(h, g), :] = part if fresh else acc[span(h, g), :] + part
+
+    def absorb_pair(i):
+        absorb([(near_slot(i), near(i)), (crossed_slot(i), crossed(i))], i // half, i == 0)
+
     build(me)
-    score(0, me)
-    for i in range(1, line):
+    score_near(0)
+    relay_keys(1)
+    take_keys(0)
+    for p in value_parts[1:]:
+        send_across(p, me)
+    score_near(1)
+    for i in range(2, line - 1):
         relay_keys(i)
-        if i > 1:
-            relay_values(i - 1)
-            score(2 * i - 3, crossed(i - 2))
-        else:
-            take_keys(0)
-            for p in value_parts[1:]:
-                send_across(p, me)
-        score(2 * i, near(i))
-        if i > 1:
-            take_keys(i - 1)
-    score(2 * line - 3, crossed(line - 2))
-    relay_values(line - 1)
-    take_keys(line - 1)
-    score(2 * line - 1, crossed(line - 1))
-
-    def settle(i, _):
-        at = pl.ds(pl.multiple_of(i * tile, 128), tile)
-        top[at, :] = jnp.broadcast_to(jnp.max(top[at, :], axis=1, keepdims=True), (tile, 128))
-        return 0
-    lax.fori_loop(0, kv_heads * blocks, settle, 0)
-    acc[...] = jnp.zeros(acc.shape, jnp.float32)
-
-    ones = jnp.ones((2 * rows, 128), jnp.bfloat16)
-
-    def value_step(i, _):
-        block, over = near(i), crossed(i)
-        for p in value_parts:
-            arrived(p, over)
+        if i == 2:
+            score_crossed(0)
+            relay_values(1)
+        cross_values(i - 1)
+        relay_values(i)
+        score_near(i)
+        take_keys(i - 1)
+        score_crossed(i - 1)
+    relay_keys(last)
+    for i in range(half - 1):
+        take_values(i)
+    settle_first()
+    cross_values(last - 1)
+    for i in range(half - 1):
+        absorb_pair(i)
+    take_keys(last - 1)
+    score_near(last)
+    relay_values(last)
+    score_crossed(last - 1)
+    cross_values(last)
+    take_values(half - 1)
+    absorb_pair(half - 1)
+    take_keys(last)
+    score_crossed(last)
+    settle_second()
+    for i in range(half, last):
+        take_values(i)
+        absorb_pair(i)
+    absorb([(near_slot(last), near(last))], 1)
+
+    att = q
+
+    def finish(g):
         for h in range(kv_heads):
-            va = jnp.concatenate([
-                jnp.concatenate([kv[2 * h + 1, pl.ds(pl.multiple_of(block * rows, 128), rows), :],
-                                 kv[2 * h + 1, pl.ds(pl.multiple_of(over * rows, 128), rows), :]],
-                                axis=0), ones], axis=1)
-            for g in range(blocks):
-                to = slice((h * blocks + g) * tile, (h * blocks + g + 1) * tile)
-                best = top[to, :]
-                weight = jnp.concatenate(
-                    [jnp.exp2(scores[2 * i + x, to, j:j + 128] - best).astype(jnp.bfloat16)
-                     for x in range(2) for j in range(0, rows, 128)], axis=1)
-                acc[to, :] += jnp.dot(weight, va, preferred_element_type=jnp.float32)
-        return 0
-    lax.fori_loop(0, line, value_step, 0)
-
-    att = q
-    for h in range(kv_heads):
-        for g in range(blocks):
+            whole = acc[span(h, g), :] + summed(h, g, [(crossed_slot(last), crossed(last))], 1)
+            res = (whole[:, :128] / whole[:, 128:]).astype(jnp.bfloat16)
             for m in range(per_kv):
-                at = ((h * blocks + g) * per_kv + m) * 128
-                res = acc[at:at + 128, :128] / acc[at:at + 128, 128:]
                 cols = (h * per_kv + m) * 128
-                att[g * 128:(g + 1) * 128, cols:cols + 128] = res.astype(jnp.bfloat16)
+                att[g * 128:(g + 1) * 128, cols:cols + 128] = res[m * 128:(m + 1) * 128]
 
     quarter = o_ref.shape[1]
     parts = quarter // wide
-    w_load.wait()
-
-    def product(group, core, j):
+
+    def product(g, group, core, j):
         cols = pl.ds(pl.multiple_of((group * 2 + core) * quarter + j * wide, 128), wide)
-        return jnp.dot(att[...], w[:, cols], preferred_element_type=jnp.float32)
-
-    def pair_copy(i, j):
+        at = pl.ds(pl.multiple_of(g * 128, 128), 128)
+        return jnp.dot(att[at, :], w[:, cols], preferred_element_type=jnp.float32)
+
+    def pair_copy(i, k):
         return pltpu.make_async_remote_copy(
-            src_ref=pair_out.at[i, j], dst_ref=pair_in.at[i, j], send_sem=pair_send.at[i, j],
-            recv_sem=pair_recv.at[i, j], device_id=partner, device_id_type=MESH)
-
-    def far_copy(i, j):
+            src_ref=pair_out.at[i, k], dst_ref=pair_in.at[i, k], send_sem=pair_send.at[i, k],
+            recv_sem=pair_recv.at[i, k], device_id=partner, device_id_type=MESH)
+
+    def far_copy(i, k):
         return pltpu.make_async_remote_copy(
-            src_ref=far_out.at[i - 1, j], dst_ref=far_in.at[i - 1, j], send_sem=far_send.at[i, j],
-            recv_sem=far_recv.at[i, j], device_id=(me, far(i) * 2 + c), device_id_type=MESH)
-
-    def far_step(k, _):
-        i, j = 1 + k // parts, lax.rem(k, parts)
-        pair_out[i, j] = product(far(i), 1 - c, j).astype(jnp.bfloat16)
-        pair_copy(i, j).start()
-        mine = product(far(i), c, j)
-        pair_copy(i, j).wait_recv()
-        far_out[i - 1, j] = (mine + pair_in[i, j].astype(jnp.float32)).astype(jnp.bfloat16)
-        far_copy(i, j).start()
+            src_ref=far_out.at[i - 1, k], dst_ref=far_in.at[i - 1, k], send_sem=far_send.at[i, k],
+            recv_sem=far_recv.at[i, k], device_id=(me, far(i) * 2 + c), device_id_type=MESH)
+
+    def lend(g, i, j):
+        k = g * parts + j
+        pair_out[i, k] = product(g, far(i), 1 - c, j).astype(jnp.bfloat16)
+        pair_copy(i, k).start()
+
+    def ship(g, i, j):
+        k = g * parts + j
+        mine = product(g, far(i), c, j)
+        pair_copy(i, k).wait_recv()
+        far_out[i - 1, k] = (mine + pair_in[i, k].astype(jnp.float32)).astype(jnp.bfloat16)
+        far_copy(i, k).start()
+
+    take_values(last)
+    trips = [(g, i, j) for g in range(blocks) for i in range(1, groups) for j in range(parts)]
+    ahead = 3
+    for s, trip in enumerate(trips):
+        if s % (len(trips) // blocks) == 0:
+            finish(trip[0])
+        if s == 0:
+            w_load.wait()
+        lend(*trip)
+        if s >= ahead:
+            ship(*trips[s - ahead])
+    for trip in trips[-ahead:]:
+        ship(*trip)
+
+    def spot(k):
+        return pl.ds(pl.multiple_of(k * 128, 128), 128)
+
+    def near_step(k, _):
+        g, j = k // parts, lax.rem(k, parts)
+        lend(g, 0, j)
+        acc[spot(k), :wide] = product(g, y, c, j)
         return 0
-    lax.fori_loop(0, (groups - 1) * parts, far_step, 0)
-
-    def near_rows(j):
-        return pl.ds(pl.multiple_of(j * rows, 128), rows)
-
-    def near_step(j, _):
-        pair_out[0, j] = product(y, 1 - c, j).astype(jnp.bfloat16)
-        pair_copy(0, j).start()
-        acc[near_rows(j), :wide] = product(y, c, j)
+    lax.fori_loop(0, blocks * parts, near_step, 0)
+
+    def close_step(k, _):
+        g, j = k // parts, lax.rem(k, parts)
+        pair_copy(0, k).wait_recv()
+        res = acc[spot(k), :wide] + pair_in[0, k].astype(jnp.float32)
+        for i in range(1, groups):
+            far_copy(i, k).wait_recv()
+            res = res + far_in[i - 1, k].astype(jnp.float32)
+        o_ref[pl.ds(pl.multiple_of(g * 128, 128), 128),
+              pl.ds(pl.multiple_of(j * wide, 128), wide)] = res.astype(jnp.bfloat16)
         return 0
-    lax.fori_loop(0, parts, near_step, 0)
-
-    def close_step(j, _):
-        pair_copy(0, j).wait_recv()
-        res = acc[near_rows(j), :wide] + pair_in[0, j].astype(jnp.float32)
-        for i in range(1, groups):
-            far_copy(i, j).wait_recv()
-            res = res + far_in[i - 1, j].astype(jnp.float32)
-        o_ref[:, pl.ds(pl.multiple_of(j * wide, 128), wide)] = res.astype(jnp.bfloat16)
-        return 0
-    lax.fori_loop(0, parts, close_step, 0)
+    lax.fori_loop(0, blocks * parts, close_step, 0)
 
     def drain(i, _):
         for p in range(2 * kv_heads + 1):
@@ -288,7 +363,7 @@
             if i:
                 far_copy(i, j).wait_send()
         return 0
-    lax.fori_loop(0, parts, drain_out, 0)
+    lax.fori_loop(0, blocks * parts, drain_out, 0)
 
 
 def shards(n, tp, queries, keys, values, out_weight, block_order):
@@ -300,15 +375,15 @@
     wide = min(256, quarter)
     parts, groups, tokens, blocks = quarter // wide, tp // 2, n * rows, rows // 128
     dims = (n, tp, rows, heads, kv_heads, wide)
-    any_space = pl.BlockSpec(memory_space=pl.ANY)
+    hbm_space = pl.BlockSpec(memory_space=pltpu.HBM)
     dma = pltpu.SemaphoreType.DMA
     bf16 = jnp.bfloat16
-    swap = pltpu.VMEM((groups, parts, rows, wide), bf16)
-    swap_far = pltpu.VMEM((groups - 1, parts, rows, wide), bf16)
+    swap = pltpu.VMEM((groups, blocks * parts, 128, wide), bf16)
+    swap_far = pltpu.VMEM((groups - 1, blocks * parts, 128, wide), bf16)
     return pl.pallas_call(
         functools.partial(kernel, dims),
         out_shape=jax.ShapeDtypeStruct((rows, quarter), bf16),
-        in_specs=[any_space] * 4 + [pl.BlockSpec(memory_space=pltpu.SMEM)],
+        in_specs=[hbm_space] * 4 + [pl.BlockSpec(memory_space=pltpu.SMEM)],
         out_specs=pl.BlockSpec(memory_space=pltpu.VMEM),
         scratch_shapes=[
             pltpu.VMEM(queries.shape, bf16),
@@ -317,16 +392,16 @@
             pltpu.VMEM((n, 8, 128), jnp.int32),
             pltpu.VMEM((blocks, tokens, 128), bf16),
             pltpu.VMEM((128, 128), bf16),
-            pltpu.VMEM((n, heads * rows, rows), jnp.float32),
-            pltpu.VMEM((heads * rows, 128), jnp.float32),
+            pltpu.VMEM((n - 3, heads * rows, rows), jnp.float32),
+            pltpu.VMEM((2, heads * rows, 128), jnp.float32),
             pltpu.VMEM((heads * rows, 256), jnp.float32),
             swap, swap, swap_far, swap_far,
             dma((2 * kv_heads + 2,)),
             dma((2 * kv_heads + 1, n, 3)), dma((2 * kv_heads + 1, n)),
-            dma((groups, parts)), dma((groups, parts)), dma((groups, parts)), dma((groups, parts)),
+            *[dma((groups, blocks * parts))] * 4,
         ],
         compiler_params=pltpu.CompilerParams(
-            collective_id=0, has_side_effects=True, vmem_limit_bytes=67043328),
+            collective_id=0, has_side_effects=True, vmem_limit_bytes=53 * 2**20),
     )(queries, keys, values, out_weight, block_order)
 
 

time: 53.3 us -> 49.9 us (0.936)
  Pallas kernels: 51.2 us -> 48.3 us
    pallas_call x1, Pallas kernels: 51.2 us -> 48.3 us  [shards(): pl.pallas_call(functools.partial(kernel, dims), out_shape=jax.ShapeDtypeS...]
    unnamed x1 -> x3, local copies, waits for them, and re-layouts: 1.87 us -> 1.45 us
where the time goes in v2:
time: 49.9 us; the launch traced here: 49.7 us
  Pallas kernels  48.3 us (97%)
  local copies, waits for them, and re-layouts  1.45 us (3%)
    pallas_call x1, Pallas kernels, shards(): pl.pallas_call(functools.partial(kernel, dims), out_shape=jax.ShapeDtypeS...  48.3 us
    unnamed x3, local copies, waits for them, and re-layouts  1.45 us

profile of v2, /device:TPU:0, one launch (start us, length us, event | category | flops | bytes accessed | tf_op | source)
XLA Modules:
  0.0 49.7 jit_solution(15500884986915108481)
XLA Ops:
  0.0 0.0 copy-start
  0.0 0.7 %copy-done = s32[2]{0:T(128)S(1)} copy-done((s32[2]{0:T(128)S(1)}, s32[2]{0:T(128)}, u32[]{:S(2)}) %copy-start) | copy-done | bytes 32
  0.7 48.3 %shard_map.55 = bf16[256,1024]{1,0:T(8,128)(2,1)S(1)} custom-call(bf16[256,2048]{1,0:T(8,128)(2,1)} %q_hbm.1, bf16[256,1024]{1,0:T(8,128)(2,1)} %k_hbm.1, bf16[256,1024]{1,0:T(8,128)(2,1)} %v_hbm.1, bf16[2048,4096]{1,0:T(8,128)(2,1)} %w_hbm.1, s32[2]{0:T(128)S(1)} %copy-done), custom_call_target="tpu_custom_call" | custom-call | tf_op jit(solution)/shard_map/pallas_call | solution.py:383
  48.9 0.8 %copy.7 = bf16[256,1024]{1,0:T(8,128)(2,1)} copy(bf16[256,1024]{1,0:T(8,128)(2,1)S(1)} %shard_map.55) | data formatting | bytes 1048576
Async XLA Ops:
  0.0 0.7 %copy-start = (s32[2]{0:T(128)S(1)}, s32[2]{0:T(128)}, u32[]{:S(2)}) copy-start(s32[2]{0:T(128)} %order.1) | copy-start | bytes 28

commit v3 on v2

--- a/solution.py
+++ b/solution.py
@@ -15,7 +15,44 @@
 NT = (((1,), (1,)), ((), ()))
 
 
-def kernel(dims, q_hbm, k_hbm, v_hbm, w_hbm, order, o_ref, q, w, kv, orders, mask, eye, scores,
+ENDS = (
+    (("own_across", 0, 1), ("keys", 1, 0), ("own_along", 0, 0), ("own_along", 0, 1), ("value", 1, 1), ("cross", 1, 1), ("own_across", 0, 0),),
+    (),
+    (),
+    (("keys", 2, 0),),
+    (),
+    (("value", 2, 0), ("cross", 2, 0),),
+    (("detour", 0, 0), ("value", 2, 1),),
+    (("keys", 3, 0),),
+    (("cross", 2, 1),),
+    (("value", 1, 0),),
+    (("value", 3, 0), ("cross", 1, 0), ("cross", 3, 0),),
+    (("value", 3, 1), ("cross", 3, 1),),
+    (),
+    (),
+    (),
+)
+INNER = (
+    (("own_across", 0, 0), ("own_along", 0, 0), ("own_along", 0, 1), ("keys", 1, 0), ("own_across", 0, 1), ("keys", 2, 0),),
+    (("value", 2, 0), ("value", 1, 0), ("value", 2, 1), ("value", 1, 1),),
+    (),
+    (("cross", 1, 1), ("cross", 1, 0), ("keys", 3, 0),),
+    (("detour", 0, 0),),
+    (("value", 3, 0), ("cross", 2, 1),),
+    (),
+    (("value", 3, 1), ("cross", 2, 0),),
+    (("cross", 3, 1),),
+    (),
+    (),
+    (("cross", 3, 0),),
+    (),
+    (),
+    (),
+)
+DETOUR = (0, )
+
+
+def kernel(dims, q_hbm, k_hbm, v_hbm, w_hbm, order_hbm, o_ref, order, q, w, kv, orders, mask, eye, scores,
            top, acc, pair_out, pair_in, far_out, far_in, load_sem, send, recv,
            pair_send, pair_recv, far_send, far_recv):
     n, tp, rows, heads, kv_heads, wide = dims
@@ -32,6 +69,22 @@
     def far(i):
         return lax.rem(y + i, groups)
 
+    def guarded(cond, act):
+        pl.when(cond)(act)
+
+    up, down, across = a + 1 < line, a > 0, a * 2 + other
+
+    barrier = pltpu.get_barrier_semaphore()
+
+    def greet(target):
+        pl.semaphore_signal(barrier, inc=1, device_id=target, device_id_type=MESH)
+
+    guarded(up, lambda: greet((me + 2, t)))
+    guarded(down, lambda: greet((me - 2, t)))
+    greet((across, t))
+    greet(partner)
+    for i in range(1, groups):
+        greet((me, far(i) * 2 + c))
     first = t * heads // (QUERY_HEADS // KEY_VALUE_HEADS)
     own = pl.ds(pl.multiple_of(me * rows, 128), rows)
     key_parts = range(0, 2 * kv_heads, 2)
@@ -44,26 +97,9 @@
         loads[p].start()
     q_load = pltpu.make_async_copy(q_hbm, q, load_sem.at[2 * kv_heads])
     w_load = pltpu.make_async_copy(w_hbm, w, load_sem.at[2 * kv_heads + 1])
-    q_load.start()
-    for i in range(blocks):
-        orders[pl.ds(me, 1), i:i + 1, :] = jnp.full((1, 1, 128), order[i], jnp.int32)
-
-    def guarded(cond, act):
-        pl.when(cond)(act)
-
-    up, down, across = a + 1 < line, a > 0, a * 2 + other
-
-    barrier = pltpu.get_barrier_semaphore()
-
-    def greet(target):
-        pl.semaphore_signal(barrier, inc=1, device_id=target, device_id_type=MESH)
-
-    guarded(up, lambda: greet((me + 2, t)))
-    guarded(down, lambda: greet((me - 2, t)))
-    greet((across, t))
-    greet(partner)
-    for i in range(1, groups):
-        greet((me, far(i) * 2 + c))
+    order_load = pltpu.make_async_copy(order_hbm, order, load_sem.at[2 * kv_heads + 2])
+    order_load.start()
+
     pl.semaphore_wait(barrier, 1 + groups + up.astype(jnp.int32) + down.astype(jnp.int32))
 
     marks = 2 * kv_heads
@@ -116,15 +152,20 @@
                 at = pl.ds(pl.multiple_of(i * rows + j * 128, 128), 128)
                 mask[g, at, :] = jnp.where(kpos <= qpos, 0.0, -1e30).astype(jnp.bfloat16)
 
-    for p in (marks, *key_parts):
-        if p != marks:
-            loads[p].wait()
+    def launch(p):
         onward(p, me)
         send_across(p, me)
+
+    for p in key_parts:
+        loads[p].wait()
+        launch(p)
+    order_load.wait()
+    for i in range(blocks):
+        orders[pl.ds(me, 1), i:i + 1, :] = jnp.full((1, 1, 128), order[i], jnp.int32)
+    launch(marks)
+    q_load.start()
     for p in value_parts:
         loads[p].wait()
-        onward(p, me)
-    send_across(1, me)
     w_load.start()
     eye[...] = (row == col).astype(jnp.bfloat16)
     q_load.wait()
@@ -162,35 +203,61 @@
                 top[side, to, :] = best
 
     def score_near(i):
+        build(near(i))
         score(near_slot(i), near(i), i // half, i % half == 0)
 
     def score_crossed(i):
+        for p in (marks, *key_parts):
+            arrived(p, crossed(i))
+        build(crossed(i))
         score(crossed_slot(i), crossed(i), i // half)
 
-    def relay_keys(i):
+    twin = a + 1 - 2 * lax.rem(a, 2)
+    detour = DETOUR if line == 4 else ()
+
+    def keys(i, _):
         for p in (marks, *key_parts):
             arrived(p, near(i))
             onward(p, near(i))
             send_across(p, near(i))
-        build(near(i))
-
-    def relay_values(i):
-        for p in value_parts:
-            arrived(p, near(i))
-            onward(p, near(i))
-
-    def cross_values(i):
-        for p in value_parts:
-            send_across(p, near(i))
-
-    def take_keys(i):
-        for p in (marks, *key_parts):
-            arrived(p, crossed(i))
-        build(crossed(i))
+
+    def value(i, h):
+        arrived(value_parts[h], near(i))
+        onward(value_parts[h], near(i))
+
+    def cross(i, h):
+        if h in detour:
+            guarded(column(i) != twin, lambda: send_across(value_parts[h], near(i)))
+        else:
+            send_across(value_parts[h], near(i))
+
+    def detoured(h):
+        block = a * 2 + other
+        return (piece(value_parts[h], block, 0, me + 2), piece(value_parts[h], block, 1, me - 2))
+
+    def detour_value(_, h):
+        arrived(value_parts[h], a * 2 + other)
+        rise, fall = detoured(h)
+        guarded(twin > a, lambda: rise.start())
+        guarded(twin < a, lambda: fall.start())
+
+    def own_across(_, h):
+        send_across(value_parts[h], me)
+
+    def own_along(_, h):
+        onward(value_parts[h], me)
+
+    acts = dict(keys=keys, value=value, cross=cross, detour=detour_value,
+                own_across=own_across, own_along=own_along)
+
+    def issue(orders_of_work):
+        for name, i, h in orders_of_work:
+            acts[name](i, h)
 
     def take_values(i):
-        for p in value_parts:
-            arrived(p, crossed(i))
+        for h, p in enumerate(value_parts):
+            if i or h not in detour:
+                arrived(p, crossed(i))
 
     def peak(side, at):
         return jnp.broadcast_to(jnp.max(top[side, at, :], axis=1, keepdims=True), (tile, 128))
@@ -231,46 +298,42 @@
                 acc[span(h, g), :] = part if fresh else acc[span(h, g), :] + part
 
     def absorb_pair(i):
+        take_values(i)
         absorb([(near_slot(i), near(i)), (crossed_slot(i), crossed(i))], i // half, i == 0)
 
-    build(me)
-    score_near(0)
-    relay_keys(1)
-    take_keys(0)
-    for p in value_parts[1:]:
-        send_across(p, me)
-    score_near(1)
-    for i in range(2, line - 1):
-        relay_keys(i)
+    heads_of = range(kv_heads)
+    every = {i: [("value", i, h) for h in heads_of] for i in range(line)}
+    over = {i: [("cross", i, h) for h in heads_of] for i in range(line)}
+    work = [([("own_across", 0, 0), *[("own_along", 0, h) for h in heads_of]], score_near, 0),
+            ([("keys", 1, 0), *[("own_across", 0, h) for h in heads_of[1:]]], score_near, 1)]
+    for i in range(2, last):
         if i == 2:
-            score_crossed(0)
-            relay_values(1)
-        cross_values(i - 1)
-        relay_values(i)
-        score_near(i)
-        take_keys(i - 1)
-        score_crossed(i - 1)
-    relay_keys(last)
-    for i in range(half - 1):
-        take_values(i)
-    settle_first()
-    cross_values(last - 1)
-    for i in range(half - 1):
-        absorb_pair(i)
-    take_keys(last - 1)
-    score_near(last)
-    relay_values(last)
-    score_crossed(last - 1)
-    cross_values(last)
-    take_values(half - 1)
-    absorb_pair(half - 1)
-    take_keys(last)
-    score_crossed(last)
-    settle_second()
-    for i in range(half, last):
-        take_values(i)
-        absorb_pair(i)
-    absorb([(near_slot(last), near(last))], 1)
+            work.append(([("keys", 2, 0)], score_crossed, 0))
+        work.append(((every[1] if i == 2 else [("keys", i, 0)]) + over[i - 1] + every[i],
+                     score_near, i))
+        work.append(([], score_crossed, i - 1))
+    work.append(([("keys", last, 0)], lambda _: settle_first(), 0))
+    work.append((over[last - 1], absorb_pair, 0))
+    work += [([], absorb_pair, i) for i in range(1, half - 1)]
+    work.append(([], score_near, last))
+    work.append((every[last], score_crossed, last - 1))
+    work.append((over[last], absorb_pair, half - 1))
+    work.append(([], score_crossed, last))
+    work.append(([], lambda _: settle_second(), 0))
+    work += [([], absorb_pair, i) for i in range(half, last)]
+    work.append(([], lambda _: absorb([(near_slot(last), near(last))], 1), 0))
+
+    at_end = jnp.logical_or(a == 0, a == last)
+    for s, (common, act, i) in enumerate(work):
+        if line == 4:
+            if ENDS[s] == INNER[s]:
+                issue(ENDS[s])
+            else:
+                guarded(at_end, lambda: issue(ENDS[s]))
+                guarded(jnp.logical_not(at_end), lambda: issue(INNER[s]))
+        else:
+            issue(common)
+        act(i)
 
     att = q
 
@@ -353,9 +416,16 @@
             blk = i * 2 + b
             guarded(jnp.logical_and(up, i <= a), lambda: piece(p, blk, 0, me + 2).wait_send())
             guarded(jnp.logical_and(down, i >= a), lambda: piece(p, blk, 1, me - 2).wait_send())
-            piece(p, blk, 2, across).wait_send()
+            if p % 2 and p // 2 in detour:
+                guarded(i != twin, lambda: piece(p, blk, 2, across).wait_send())
+            else:
+                piece(p, blk, 2, across).wait_send()
         return 0
     lax.fori_loop(0, line, drain, 0)
+    for h in detour:
+        rise, fall = detoured(h)
+        guarded(twin > a, lambda: rise.wait_send())
+        guarded(twin < a, lambda: fall.wait_send())
 
     def drain_out(j, _):
         for i in range(groups):
@@ -383,9 +453,10 @@
     return pl.pallas_call(
         functools.partial(kernel, dims),
         out_shape=jax.ShapeDtypeStruct((rows, quarter), bf16),
-        in_specs=[hbm_space] * 4 + [pl.BlockSpec(memory_space=pltpu.SMEM)],
+        in_specs=[hbm_space] * 5,
         out_specs=pl.BlockSpec(memory_space=pltpu.VMEM),
         scratch_shapes=[
+            pltpu.SMEM(block_order.shape, jnp.int32),
             pltpu.VMEM(queries.shape, bf16),
             pltpu.VMEM(out_weight.shape, bf16),
             pltpu.VMEM((2 * kv_heads, tokens, HEAD_SIZE), bf16),
@@ -396,7 +467,7 @@
             pltpu.VMEM((2, heads * rows, 128), jnp.float32),
             pltpu.VMEM((heads * rows, 256), jnp.float32),
             swap, swap, swap_far, swap_far,
-            dma((2 * kv_heads + 2,)),
+            dma((2 * kv_heads + 3,)),
             dma((2 * kv_heads + 1, n, 3)), dma((2 * kv_heads + 1, n)),
             *[dma((groups, blocks * parts))] * 4,
         ],

time: 49.9 us -> 49.2 us (0.986)
  Pallas kernels: 48.3 us -> 47.6 us
    pallas_call x1, Pallas kernels: 48.3 us -> 47.6 us  [shards(): pl.pallas_call(functools.partial(kernel, dims), out_shape=jax.ShapeDtypeS...]
where the time goes in v3:
time: 49.2 us; the launch traced here: 49.1 us
  Pallas kernels  47.6 us (97%)
  local copies, waits for them, and re-layouts  1.45 us (3%)
    pallas_call x1, Pallas kernels, shards(): pl.pallas_call(functools.partial(kernel, dims), out_shape=jax.ShapeDtypeS...  47.6 us
    unnamed x3, local copies, waits for them, and re-layouts  1.45 us

profile of v3, /device:TPU:0, one launch (start us, length us, event | category | flops | bytes accessed | tf_op | source)
XLA Modules:
  0.0 49.1 jit_solution(2004480734516251765)
XLA Ops:
  0.0 0.0 copy-start
  0.0 0.7 %copy-done = s32[2]{0:T(128)S(1)} copy-done((s32[2]{0:T(128)S(1)}, s32[2]{0:T(128)}, u32[]{:S(2)}) %copy-start) | copy-done | bytes 32
  0.7 47.6 %shard_map.55 = bf16[256,1024]{1,0:T(8,128)(2,1)S(1)} custom-call(bf16[256,2048]{1,0:T(8,128)(2,1)} %q_hbm.1, bf16[256,1024]{1,0:T(8,128)(2,1)} %k_hbm.1, bf16[256,1024]{1,0:T(8,128)(2,1)} %v_hbm.1, bf16[2048,4096]{1,0:T(8,128)(2,1)} %w_hbm.1, s32[2]{0:T(128)S(1)} %copy-done), custom_call_target="tpu_custom_call" | custom-call | tf_op jit(solution)/shard_map/pallas_call | solution.py:453
  48.3 0.8 %copy.7 = bf16[256,1024]{1,0:T(8,128)(2,1)} copy(bf16[256,1024]{1,0:T(8,128)(2,1)S(1)} %shard_map.55) | data formatting | bytes 1048576
Async XLA Ops:
  0.0 0.7 %copy-start = (s32[2]{0:T(128)S(1)}, s32[2]{0:T(128)}, u32[]{:S(2)}) copy-start(s32[2]{0:T(128)} %order_hbm.1) | copy-start | bytes 28

commit v4 on v3

--- a/solution.py
+++ b/solution.py
@@ -153,8 +153,8 @@
                 mask[g, at, :] = jnp.where(kpos <= qpos, 0.0, -1e30).astype(jnp.bfloat16)
 
     def launch(p):
+        send_across(p, me)
         onward(p, me)
-        send_across(p, me)
 
     for p in key_parts:
         loads[p].wait()
@@ -216,10 +216,10 @@
     detour = DETOUR if line == 4 else ()
 
     def keys(i, _):
-        for p in (marks, *key_parts):
+        for p in (*key_parts, marks):
             arrived(p, near(i))
+            send_across(p, near(i))
             onward(p, near(i))
-            send_across(p, near(i))
 
     def value(i, h):
         arrived(value_parts[h], near(i))

time: 49.2 us -> 48.7 us (0.990)
  Pallas kernels: 47.6 us -> 47.1 us
where the time goes in v4:
time: 48.7 us; the launch traced here: 48.6 us
  Pallas kernels  47.1 us (97%)
  local copies, waits for them, and re-layouts  1.45 us (3%)
    pallas_call x1, Pallas kernels, shards(): pl.pallas_call(functools.partial(kernel, dims), out_shape=jax.ShapeDtypeS...  47.1 us
    unnamed x3, local copies, waits for them, and re-layouts  1.45 us

profile of v4, /device:TPU:0, one launch (start us, length us, event | category | flops | bytes accessed | tf_op | source)
XLA Modules:
  0.0 48.6 jit_solution(6869213905737241661)
XLA Ops:
  0.0 0.0 copy-start
  0.0 0.7 %copy-done = s32[2]{0:T(128)S(1)} copy-done((s32[2]{0:T(128)S(1)}, s32[2]{0:T(128)}, u32[]{:S(2)}) %copy-start) | copy-done | bytes 32
  0.7 47.1 %shard_map.55 = bf16[256,1024]{1,0:T(8,128)(2,1)S(1)} custom-call(bf16[256,2048]{1,0:T(8,128)(2,1)} %q_hbm.1, bf16[256,1024]{1,0:T(8,128)(2,1)} %k_hbm.1, bf16[256,1024]{1,0:T(8,128)(2,1)} %v_hbm.1, bf16[2048,4096]{1,0:T(8,128)(2,1)} %w_hbm.1, s32[2]{0:T(128)S(1)} %copy-done), custom_call_target="tpu_custom_call" | custom-call | tf_op jit(solution)/shard_map/pallas_call | solution.py:453
  47.8 0.8 %copy.7 = bf16[256,1024]{1,0:T(8,128)(2,1)} copy(bf16[256,1024]{1,0:T(8,128)(2,1)S(1)} %shard_map.55) | data formatting | bytes 1048576
Async XLA Ops:
  0.0 0.7 %copy-start = (s32[2]{0:T(128)S(1)}, s32[2]{0:T(128)}, u32[]{:S(2)}) copy-start(s32[2]{0:T(128)} %order_hbm.1) | copy-start | bytes 28
